TPU v7x, 32 devices: a whole 2x2x4 slice. The times are simulated.
32 devices in a mesh: members: 2 (over y), elem: 4 (over z), lev: 4 (over x, core).
Axes of the slice: x: 2, y: 2, z: 4, core: 2. Of those that a mesh axis runs over, the one named last changes fastest.
Arguments:
- tracers: float32 [25, 8, 16, 2048], P(None, 'lev', None, ('members', 'elem')), parts along dimension 3, may hold values from -6 to 6
- layer_mass: float32 [8, 16, 2048], P('lev', None, ('members', 'elem')), parts along dimension 2, may hold values from 0.3 to 2.7
- winds: float32 [2, 8, 16, 2048], P(None, 'lev', None, ('members', 'elem')), parts along dimension 3, may hold values from 0.5 to 1.5
- metric: float32 [16, 1024], P(None, 'elem'), may hold values from 0.6 to 1.6
- neighbours: int32 [1024, 8], P('elem'), may hold values from 0 to 1023, as said below
Outputs:
- tracers_out: float32 [25, 8, 16, 2048], P(None, 'lev', None, ('members', 'elem')), parts along dimension 3
- surface: float32 [16, 2048], P(None, ('members', 'elem')), parts along dimension 1
There are 2 independent parts, one for each index of `members`. A program takes and returns all parts, laid end to end along the dimension named above; an argument that names none is the same for every part. Nothing has to cross between parts.
Inputs may be any that keep to these rules, and one draw needn't show every extreme that they name: `neighbours`: the grid has 32 columns and 32 rows of elements; it is periodic north to south, and east of column 31 of row y lies column 0 of row y + 16 (rows modulo 32). Block b of 256 elements along elem is the square patch of 16 by 16 elements in patch row b // 2 and patch column b % 2, its elements in a drawn order; so the east, west, north and south patches of block b are blocks b + 1, b - 1, b + 2, b - 2 and the diagonal ones b + 3, b + 1, b - 1, b - 2 - 1 (all modulo the number of blocks). Adjacency is symmetric.
All inputs are finite; a program needn't handle non-finite values.
Results may differ from a plain program's by a relative error of at most 0.0003.
Values sent between devices are 32-bit elements; how exact they have to be, the bound alone decides.
A program may use at most 128 MiB of HBM per device.

v0:
```python
import math

import jax
import jax.numpy as jnp
import numpy as np
from jax import lax
from jax.sharding import PartitionSpec as P

PSIDE = 16


time_step = 0.035


def shifted(block, axis, distance):
    devices = range(lax.axis_size(axis))
    route = [((i - distance) % len(devices), i) for i in devices]
    return lax.ppermute(block, axis, route)


def prefix(part, axis, combine, identity):
    place = lax.axis_index(axis)
    gathered = lax.all_gather(part, axis)
    state = jnp.zeros_like(part) + jnp.asarray(identity, part.dtype)

    def one(turn, state):
        return combine(state, lax.dynamic_index_in_dim(gathered, turn, 0, False))

    return lax.fori_loop(0, place, one, state)


def extended_2(cells, sides, width):
    for axis, dim in sides:
        count = lax.axis_size(axis)
        ends = count - 1
        head = lax.slice_in_dim(cells, 0, width, axis=dim)
        tail = lax.slice_in_dim(cells, cells.shape[dim] - width, cells.shape[dim], axis=dim)
        cells = jnp.concatenate(
            [
                lax.ppermute(tail, axis, [(i, (i + 1) % count) for i in range(ends)]),
                cells,
                lax.ppermute(head, axis, [((i + 1) % count, i) for i in range(ends)]),
            ],
            axis=dim,
        )
    return cells


def lagrange_scale(points, which):
    product = 1.0
    for other in range(4):
        if other != which:
            product = product * (points[which] - points[other])
    return product


def node_tables():
    points = np.array([-1.0, -1.0 / math.sqrt(5.0), 1.0 / math.sqrt(5.0), 1.0])
    weights = np.array([1.0, 5.0, 5.0, 1.0]) / 6.0
    derivative = np.zeros((4, 4))
    for target in range(4):
        for source in range(4):
            if target == source:
                derivative[target, source] = sum(
                    (
                        1.0 / (points[target] - points[other])
                        for other in range(4)
                        if other != target
                    )
                )
            else:
                derivative[target, source] = lagrange_scale(points, target) / (
                    lagrange_scale(points, source) * (points[target] - points[source])
                )
    return (
        np.kron(np.eye(4), derivative),
        np.kron(derivative, np.eye(4)),
        np.kron(weights, weights),
    )


def side_links():
    column = list(range(4))
    return [
        ([4 * step + 3 for step in column], [4 * step for step in column]),
        ([4 * step for step in column], [4 * step + 3 for step in column]),
        ([12 + step for step in column], [step for step in column]),
        ([step for step in column], [12 + step for step in column]),
        ([15], [0]),
        ([12], [3]),
        ([3], [12]),
        ([0], [15]),
    ]


def link_table():
    table = np.zeros((8, 16, 16), np.float32)
    for direction, pair in enumerate(side_links()):
        for target, source in zip(pair[0], pair[1]):
            table[direction, source, target] = 1.0
    return table


def apply_table(table, field):
    return jnp.einsum(
        "nm,...me->...ne", jnp.asarray(table, jnp.float32), field, precision=lax.Precision.HIGHEST
    )


def tendency(state, winds, metric):
    along_east, along_north, weights = node_tables()
    east_flux = metric * winds[0] * state
    north_flux = metric * winds[1] * state
    return -(apply_table(along_east, east_flux) + apply_table(along_north, north_flux)) / metric


def assemble_rows(rows, extended, positions):
    flat_index = jnp.transpose(positions).reshape(-1)
    picked = jnp.take(extended, flat_index, axis=0).reshape((8,) + rows.shape)
    placed = jnp.einsum(
        "dwfm,dmn->wfn", picked, jnp.asarray(link_table()), precision=lax.Precision.HIGHEST
    )
    return rows + placed


def pack_order(flags, slots):
    ranks = jnp.cumsum(flags.astype(jnp.int32)) - 1
    match = flags[:, None] & (ranks[:, None] == jnp.arange(slots, dtype=jnp.int32)[None, :])
    return jnp.sum(
        jnp.where(match, jnp.arange(flags.shape[0], dtype=jnp.int32)[:, None], 0), axis=0
    )


def referenced(within, chosen, width):
    found = (within[:, :, None] == jnp.arange(width, dtype=jnp.int32)[None, None, :]) & chosen[
        :, :, None
    ]
    return jnp.any(found, axis=(0, 1)).astype(jnp.int32)


def per_device(tracers, layer_mass, winds, metric, neighbours):
    width = metric.shape[-1]
    count = lax.axis_size("elem")
    place = lax.axis_index("elem")
    across = min(8, max(2, count // 8))
    weights = node_tables()[2]
    mass = jnp.asarray(weights, jnp.float32)[:, None] * metric
    owner = neighbours // width
    within = neighbours % width
    relation = (owner - place) % count
    roles = [
        (1, PSIDE),
        (-1, PSIDE),
        (across, PSIDE),
        (-across, PSIDE),
        (across + 1, 1),
        (across - 1, 1),
        (1 - across, 1),
        (-1 - across, 1),
    ]
    slot_sizes = {}
    for offset, amount in roles:
        key_rel = offset % count
        slot_sizes[key_rel] = slot_sizes.get(key_rel, 0) + amount
    peers = sorted(slot_sizes.keys())
    orders = []
    positions = within
    start = width
    for peer in peers:
        slots = min(slot_sizes[peer], width)
        orders.append(
            (peer, pack_order(jnp.any(relation == (count - peer) % count, axis=1), slots))
        )
        rank = jnp.cumsum(referenced(within, relation == peer, width)) - 1
        positions = jnp.where(relation == peer, start + rank[within], positions)
        start = start + slots

    def extend(rows):
        pieces = [rows]
        for peer, order in orders:
            packed = jnp.take(rows, order, axis=0)
            pieces.append(shifted(packed, "elem", -peer))
        return jnp.concatenate(pieces, axis=0)

    start_state = jnp.concatenate([layer_mass[None], tracers * layer_mass[None]], axis=0)
    first_rate = tendency(start_state, winds, metric)
    first_flat = jnp.concatenate(
        [mass[None], (mass * first_rate).reshape((-1,) + first_rate.shape[2:])], axis=0
    )
    first_rows = jnp.transpose(first_flat, (2, 0, 1))
    first_sum = jnp.transpose(assemble_rows(first_rows, extend(first_rows), positions), (1, 2, 0))
    shared = first_sum[0]
    middle_state = start_state + time_step * (first_sum[1:] / shared).reshape(first_rate.shape)
    second_rate = tendency(middle_state, winds, metric)
    second_flat = (mass * second_rate).reshape((-1,) + second_rate.shape[2:])
    second_rows = jnp.transpose(second_flat, (2, 0, 1))
    second_sum = jnp.transpose(
        assemble_rows(second_rows, extend(second_rows), positions), (1, 2, 0)
    )
    final_state = 0.5 * (
        start_state + middle_state + time_step * (second_sum / shared).reshape(second_rate.shape)
    )
    thick = final_state[0]
    carried = final_state[1:]
    levels_here = thick.shape[0]
    total_levels = levels_here * lax.axis_size("lev")
    column = jnp.sum(thick, axis=0)
    below_sum = prefix(column, "lev", jnp.add, jnp.zeros_like(column))
    surface = lax.psum(column, "lev")
    edges = (
        lax.axis_index("lev") * levels_here + jnp.arange(levels_here + 1, dtype=jnp.int32)
    ).astype(jnp.float32)
    fraction = (edges + edges * (edges - 1.0) / (total_levels - 1)) / (2.0 * total_levels)
    layers = edges[:-1]
    share = (1.0 + 2.0 * layers / (total_levels - 1)) / (2.0 * total_levels)
    above_mass = below_sum[None] + jnp.concatenate(
        [jnp.zeros_like(column)[None], jnp.cumsum(thick, axis=0)], axis=0
    )
    delta = above_mass - surface * fraction[:, None, None]
    ratio = carried / thick
    padded = extended_2(ratio, (("lev", 1),), 1)
    flux = delta * jnp.where(delta > 0.0, padded[:, :-1], padded[:, 1:])
    result = (carried + flux[:, :-1] - flux[:, 1:]) / (surface * share[:, None, None])
    return (result, surface)


def solution(mesh):
    placed = (
        P(None, "lev", None, ("members", "elem")),
        P("lev", None, ("members", "elem")),
        P(None, "lev", None, ("members", "elem")),
        P(None, "elem"),
        P("elem", None),
    )
    return jax.shard_map(
        per_device,
        mesh=mesh,
        in_specs=placed,
        out_specs=(P(None, "lev", None, ("members", "elem")), P(None, ("members", "elem"))),
        check_vma=False,
    )
```

profile of v0, /device:TPU:1, one launch (start us, length us, event | category | flops | bytes accessed | tf_op | source)
XLA Modules:
  0.0 240.9 jit_solution(2680610831793723177)
XLA Ops:
  4.3 1.3 broadcast_multiply_fusion
  8.5 1.4 copy.70
  11.6 1.8 broadcast_select_fusion.2
  13.4 3.1 %collective-permute-start.1 = (f32[32,53,16]{0,2,1:T(8,128)}, f32[32,53,16]{0,2,1:T(8,128)}, u32[]{:S(2)}, u32[]{:S(2)}) collective-permute-start(f32[32,53,16]{0,2,1:T(8,128)} %broadcast_select_fusion.2), channel_id=1, source_target_pairs={{8,0},{12,4},{0,8},{4,12},{9,1},{13,5},{1,9},{5,13},{10,2},{14,6},... | collective-permute-start | bytes 325640 | tf_op jit(solution)/shard_map/ppermute | solution.py:18
  18.9 1.8 broadcast_select_fusion
  20.7 1.3 collective-permute-start.2
  23.8 2.2 collective-permute-start
  26.0 1.4 fusion.13
  28.2 13.1 %gather_fusion.1 = s32[2048]{0:T(1024)S(1)} fusion(s32[256]{0:T(256)S(1)} %add_bitcast_fusion.4, s32[2048]{0:T(1024)S(1)} %broadcast_clamp_fusion.1), kind=kCustom, calls=%fused_computation.5 | custom fusion | bytes 24576 | tf_op jit(solution)/shard_map/gather | solution.py:175
  42.1 13.1 %gather_fusion.2 = s32[2048]{0:T(1024)S(1)} fusion(s32[256]{0:T(256)S(1)} %add_bitcast_fusion.3, s32[2048]{0:T(1024)S(1)} %broadcast_clamp_fusion.1), kind=kCustom, calls=%fused_computation.6 | custom fusion | bytes 24576 | tf_op jit(solution)/shard_map/gather | solution.py:175
  56.0 13.1 %gather_fusion = s32[2048]{0:T(1024)S(1)} fusion(s32[256]{0:T(256)S(1)} %add_bitcast_fusion.5, s32[2048]{0:T(1024)S(1)} %broadcast_clamp_fusion.1), kind=kCustom, calls=%fused_computation.4 | custom fusion | bytes 24576 | tf_op jit(solution)/shard_map/gather | solution.py:175
  69.6 2.5 %pad_maximum_fusion = f32[324,53,16]{0,2,1:T(8,128)} fusion(f32[18,53,16]{0,2,1:T(8,128)} %collective-permute-done.2, f32[32,53,16]{0,2,1:T(8,128)} %collective-permute-done.1, f32[18,53,16]{0,2,1:T(8,128)S(1)} %collective-permute-done, f32[256,53,16]{0,2,1:T(8,128)S(1)} %fusion.49), kind=kLoop, calls=%fused_computation.39 | loop fusion | flops 824256 | bytes 2198016 | tf_op jit(solution)/shard_map/concatenate | solution.py:183
  72.1 2.4 copy.77
  74.4 20.7 %gather_fusion.4 = f32[2048,53,16]{1,2,0:T(8,128)} fusion(f32[324,53,16]{1,2,0:T(8,128)S(1)} %copy.77, s32[2048]{0:T(1024)S(1)} %broadcast_clamp_fusion), kind=kCustom, calls=%fused_computation.8 | custom fusion | bytes 13901824 | tf_op jit(solution)/shard_map/jit(_take)/gather | solution.py:119
  95.2 14.9 %copy.78 = f32[8,256,53,16]{1,3,0,2:T(8,128)} copy(f32[8,256,53,16]{2,3,1,0:T(8,128)} %bitcast.107) | data formatting | bytes 13893632 | tf_op jit(solution)/shard_map/jit(_take)/gather | solution.py:119
  110.1 6.1 %fusion.28 = f32[53,16,256]{2,1,0:T(8,128)S(1)} fusion(f32[8,16,16,1]{1,2,0,3:T(8,128)S(1)} %copy-done.12, f32[8,256,53,16]{1,3,0,2:T(8,128)} %copy.78, pred[8,256]{1,0:T(8,128)(4,1)S(1)} %copy.69, f32[52,16,256]{2,1,0:T(8,128)S(1)} %bitcast.115, f32[1,16,256]{2,1,0:T(8,128)S(1)} %copy-done.15), kind=kOutput, calls=%fused_computation.40 | convolution fusion | flops 335618048 | bytes 8693760 | tf_op jit(solution)/shard_map/dwfm,dmn->wfn/dot_general | solution.py:120
  118.4 1.9 fusion.20
  120.3 2.6 %copy.80 = f32[256,52,16]{1,2,0:T(8,128)S(1)} copy(f32[256,52,16]{0,2,1:T(8,128)} %bitcast.108) | data formatting | bytes 1703936 | tf_op jit(solution)/shard_map/transpose | solution.py:196
  128.0 7.7 %collective-permute-done.3 = f32[18,52,16]{0,2,1:T(8,128)} collective-permute-done((f32[18,52,16]{0,2,1:T(8,128)S(1)}, f32[18,52,16]{0,2,1:T(8,128)}, u32[]{:S(2)}, u32[]{:S(2)}) %collective-permute-start.3) | collective-permute-done | bytes 59936 | tf_op jit(solution)/shard_map/ppermute | solution.py:18
  135.7 17.2 %collective-permute-done.5 = f32[18,52,16]{0,2,1:T(8,128)S(1)} collective-permute-done((f32[18,52,16]{0,2,1:T(8,128)S(1)}, f32[18,52,16]{0,2,1:T(8,128)S(1)}, u32[]{:S(2)}, u32[]{:S(2)}) %collective-permute-start.5) | collective-permute-done | bytes 59936 | tf_op jit(solution)/shard_map/ppermute | solution.py:18
  152.9 9.2 %collective-permute-done.4 = f32[32,52,16]{0,2,1:T(8,128)} collective-permute-done((f32[32,52,16]{0,2,1:T(8,128)S(1)}, f32[32,52,16]{0,2,1:T(8,128)}, u32[]{:S(2)}, u32[]{:S(2)}) %collective-permute-start.4) | collective-permute-done | bytes 106528 | tf_op jit(solution)/shard_map/ppermute | solution.py:18
  162.0 2.5 %pad_maximum_fusion.1 = f32[324,52,16]{0,2,1:T(8,128)} fusion(f32[18,52,16]{0,2,1:T(8,128)S(1)} %collective-permute-done.5, f32[32,52,16]{0,2,1:T(8,128)} %collective-permute-done.4, f32[18,52,16]{0,2,1:T(8,128)} %collective-permute-done.3, f32[256,52,16]{0,2,1:T(8,128)S(1)} %bitcast.109), kind=kLoop, calls=%fused_computation.42 | loop fusion | flops 808704 | bytes 2156544 | tf_op jit(solution)/shard_map/concatenate | solution.py:183
  164.5 2.3 copy.86
  166.9 20.7 %gather_fusion.6 = f32[2048,52,16]{1,2,0:T(8,128)} fusion(f32[324,52,16]{1,2,0:T(8,128)S(1)} %copy.86, s32[2048]{0:T(1024)S(1)} %broadcast_clamp_fusion), kind=kCustom, calls=%fused_computation.10 | custom fusion | bytes 13639680 | tf_op jit(solution)/shard_map/jit(_take)/gather | solution.py:119
  187.6 14.9 %copy.87 = f32[8,256,52,16]{1,3,0,2:T(8,128)} copy(f32[8,256,52,16]{2,3,1,0:T(8,128)} %bitcast.106) | data formatting | bytes 13631488 | tf_op jit(solution)/shard_map/jit(_take)/gather | solution.py:119
  202.5 6.0 %fusion.38 = f32[52,16,256]{2,1,0:T(8,128)S(1)} fusion(f32[52,16,256]{2,1,0:T(8,128)S(1)} %bitcast.110, f32[8,16,16,1]{1,2,0,3:T(8,128)S(1)} %copy-done.13, f32[8,256,52,16]{1,3,0,2:T(8,128)} %copy.87, pred[8,256]{1,0:T(8,128)(4,1)S(1)} %copy.69, f32[16,256]{1,0:T(8,128)S(1)} %slice_bitcast_fusion.1), kind=kOutput, calls=%fused_computation.46 | convolution fusion | flops 329498624 | bytes 8546304 | tf_op jit(solution)/shard_map/dwfm,dmn->wfn/dot_general | solution.py:120
  208.9 7.4 %all-gather = f32[64,256]{1,0:T(8,128)S(1)} all-gather(f32[16,256]{1,0:T(8,128)S(1)} %get-tuple-element.52), channel_id=2, replica_groups=mesh['members'=2,'elem'=4,'lev'=4] {'lev'}, dimensions={0}, use_global_device_ids=true | all-gather | bytes 81920 | tf_op jit(solution)/shard_map/all_gather | solution.py:23
  216.3 9.4 %psum.7 = f32[16,256]{1,0:T(8,128)S(1)} all-reduce(f32[16,256]{1,0:T(8,128)S(1)} %get-tuple-element.52), channel_id=1, replica_groups=mesh['members'=2,'elem'=4,'lev'=4] {'lev'}, use_global_device_ids=true, to_apply=%region_25.28 | all-reduce | flops 4096 | bytes 32768 | tf_op jit(solution)/shard_map/psum | solution.py:209
  226.0 4.2 %collective-permute-start.6 = (f32[25,1,16,256]{3,2,1,0:T(8,128)S(1)}, f32[25,1,16,256]{3,2,1,0:T(8,128)S(1)}, u32[]{:S(2)}, u32[]{:S(2)}) collective-permute-start(f32[25,1,16,256]{3,2,1,0:T(8,128)S(1)} %get-tuple-element.55), channel_id=1, source_target_pairs={{0,1},{1,2},{2,3},{4,5},{5,6},{6,7},{8,9},{9,10},{10,11},{12,13},{... | collective-permute-start | bytes 1228808 | tf_op jit(solution)/shard_map/ppermute | solution.py:40
  230.2 1.9 collective-permute-start.7
  232.3 2.8 %collective-permute-done.6 = f32[25,1,16,256]{3,2,1,0:T(8,128)S(1)} collective-permute-done((f32[25,1,16,256]{3,2,1,0:T(8,128)S(1)}, f32[25,1,16,256]{3,2,1,0:T(8,128)S(1)}, u32[]{:S(2)}, u32[]{:S(2)}) %collective-permute-start.6) | collective-permute-done | bytes 409632 | tf_op jit(solution)/shard_map/ppermute | solution.py:40
  235.1 4.4 %collective-permute-done.7 = f32[25,1,16,256]{3,2,1,0:T(8,128)S(1)} collective-permute-done((f32[25,1,16,256]{3,2,1,0:T(8,128)S(1)}, f32[25,1,16,256]{3,2,1,0:T(8,128)S(1)}, u32[]{:S(2)}, u32[]{:S(2)}) %collective-permute-start.7) | collective-permute-done | bytes 409632 | tf_op jit(solution)/shard_map/ppermute | solution.py:42
  (181 shorter events, 23.8 us)
Async XLA Ops:
  0.6 5.0 %copy-start.19 = (f32[16,16,1,1]{1,0,3,2:T(8,128)S(1)}, f32[16,16,1,1]{1,0,3,2:T(8,128)}, u32[]{:S(2)}) copy-start(f32[16,16,1,1]{1,0,3,2:T(8,128)} %constant.201) | copy-start | bytes 3076
  0.6 5.0 %copy-start.8 = (f32[2,16,256]{2,1,0:T(8,128)S(1)}, f32[2,16,256]{2,1,0:T(8,128)}, u32[]{:S(2)}) copy-start(f32[2,16,256]{2,1,0:T(8,128)} %param.19) | copy-start | bytes 98308
  1.5 5.0 %copy-start.17 = (f32[16,256]{1,0:T(8,128)S(1)}, f32[16,256]{1,0:T(8,128)}, u32[]{:S(2)}) copy-start(f32[16,256]{1,0:T(8,128)} %param.21) | copy-start | bytes 49156
  1.5 5.0 %copy-start.34 = (f32[16,16,1,1]{1,0,3,2:T(8,128)S(1)}, f32[16,16,1,1]{1,0,3,2:T(8,128)}, u32[]{:S(2)}) copy-start(f32[16,16,1,1]{1,0,3,2:T(8,128)} %constant.202) | copy-start | bytes 3076
  2.7 8.9 %copy-start.28 = (pred[32]{0:T(512)(128)(4,1)}, pred[32]{0:T(512)(128)(4,1)S(1)}, u32[]{:S(2)}) copy-start(pred[32]{0:T(512)(128)(4,1)S(1)} %compare_and_fusion.3) | copy-start | bytes 100
  2.7 7.2 %copy-start.27 = (s32[1024]{0:T(1024)}, s32[1024]{0:T(1024)S(1)}, u32[]{:S(2)}) copy-start(s32[1024]{0:T(1024)S(1)} %pad_clamp_fusion.1) | copy-start | bytes 12292
  3.5 4.0 %copy-start.21 = (f32[2,16,256]{2,1,0:T(8,128)}, f32[2,16,256]{2,1,0:T(8,128)S(1)}, u32[]{:S(2)}) copy-start(f32[2,16,256]{2,1,0:T(8,128)S(1)} %get-tuple-element.58) | copy-start | bytes 98308
  4.3 3.2 %copy-start.14 = (f32[1,16,256]{2,1,0:T(8,128)}, f32[1,16,256]{2,1,0:T(8,128)S(1)}, u32[]{:S(2)}) copy-start(f32[1,16,256]{2,1,0:T(8,128)S(1)} %get-tuple-element.60) | copy-start | bytes 49156
  13.4 56.2 %collective-permute-start.1 = (f32[32,53,16]{0,2,1:T(8,128)}, f32[32,53,16]{0,2,1:T(8,128)}, u32[]{:S(2)}, u32[]{:S(2)}) collective-permute-start(f32[32,53,16]{0,2,1:T(8,128)} %broadcast_select_fusion.2), channel_id=1, source_target_pairs={{8,0},{12,4},{0,8},{4,12},{9,1},{13,5},{1,9},{5,13},{10,2},{14,6},... | collective-permute-start | bytes 325640 | tf_op jit(solution)/shard_map/ppermute | solution.py:18
  17.3 4.8 %copy-start.30 = (pred[18]{0:T(512)(128)(4,1)}, pred[18]{0:T(512)(128)(4,1)S(1)}, u32[]{:S(2)}) copy-start(pred[18]{0:T(512)(128)(4,1)S(1)} %compare_and_fusion.1) | copy-start | bytes 58
  17.3 4.7 %copy-start.25 = (s32[1024]{0:T(1024)}, s32[1024]{0:T(1024)S(1)}, u32[]{:S(2)}) copy-start(s32[1024]{0:T(1024)S(1)} %pad_clamp_fusion) | copy-start | bytes 12292
  20.7 48.8 %collective-permute-start.2 = (f32[18,53,16]{0,2,1:T(8,128)}, f32[18,53,16]{0,2,1:T(8,128)}, u32[]{:S(2)}, u32[]{:S(2)}) collective-permute-start(f32[18,53,16]{0,2,1:T(8,128)} %broadcast_select_fusion), channel_id=1, source_target_pairs={{12,0},{0,4},{4,8},{8,12},{13,1},{1,5},{5,9},{9,13},{14,2},{2,6},{... | collective-permute-start | bytes 183176 | tf_op jit(solution)/shard_map/ppermute | solution.py:18
  22.8 4.7 %copy-start.32 = (pred[18]{0:T(512)(128)(4,1)}, pred[18]{0:T(512)(128)(4,1)S(1)}, u32[]{:S(2)}) copy-start(pred[18]{0:T(512)(128)(4,1)S(1)} %compare_and_fusion.2) | copy-start | bytes 58
  22.8 5.1 %copy-start.26 = (s32[1024]{0:T(1024)}, s32[1024]{0:T(1024)S(1)}, u32[]{:S(2)}) copy-start(s32[1024]{0:T(1024)S(1)} %pad_clamp_fusion.2) | copy-start | bytes 12292
  23.8 45.8 %collective-permute-start = (f32[18,53,16]{0,2,1:T(8,128)S(1)}, f32[18,53,16]{0,2,1:T(8,128)S(1)}, u32[]{:S(2)}, u32[]{:S(2)}) collective-permute-start(f32[18,53,16]{0,2,1:T(8,128)S(1)} %broadcast_select_fusion.1), channel_id=1, source_target_pairs={{4,0},{8,4},{12,8},{0,12},{5,1},{9,5},{13,9},{1,13},{6,2},{10,6},{... | collective-permute-start | bytes 183176 | tf_op jit(solution)/shard_map/ppermute | solution.py:18
  95.1 15.0 %copy-start.7 = (f32[26,2,16,256]{3,2,1,0:T(8,128)S(1)}, f32[26,2,16,256]{3,2,1,0:T(8,128)}, u32[]{:S(2)}) copy-start(f32[26,2,16,256]{3,2,1,0:T(8,128)} %copy-done.6) | copy-start | bytes 2555908
  95.2 15.0 %copy-start.12 = (f32[8,16,16,1]{1,2,0,3:T(8,128)S(1)}, f32[8,16,16,1]{1,2,0,3:T(8,128)}, u32[]{:S(2)}) copy-start(f32[8,16,16,1]{1,2,0,3:T(8,128)} %constant.203) | copy-start | bytes 24580
  95.2 15.0 %copy-start.15 = (f32[1,16,256]{2,1,0:T(8,128)S(1)}, f32[1,16,256]{2,1,0:T(8,128)}, u32[]{:S(2)}) copy-start(f32[1,16,256]{2,1,0:T(8,128)} %copy-done.14) | copy-start | bytes 49156
  110.1 6.3 %copy-start.9 = (f32[2,16,256]{2,1,0:T(8,128)S(1)}, f32[2,16,256]{2,1,0:T(8,128)}, u32[]{:S(2)}) copy-start(f32[2,16,256]{2,1,0:T(8,128)} %param.19) | copy-start | bytes 98308
  110.1 6.3 %copy-start.11 = (f32[2,16,256]{2,1,0:T(8,128)S(1)}, f32[2,16,256]{2,1,0:T(8,128)}, u32[]{:S(2)}) copy-start(f32[2,16,256]{2,1,0:T(8,128)} %copy-done.10) | copy-start | bytes 98308
  110.1 6.3 %copy-start.20 = (f32[16,16,1,1]{1,0,3,2:T(8,128)S(1)}, f32[16,16,1,1]{1,0,3,2:T(8,128)}, u32[]{:S(2)}) copy-start(f32[16,16,1,1]{1,0,3,2:T(8,128)} %constant.201) | copy-start | bytes 3076
  116.4 3.9 %copy-start.4 = (f32[52,16,256]{2,1,0:T(8,128)}, f32[52,16,256]{2,1,0:T(8,128)S(1)}, u32[]{:S(2)}) copy-start(f32[52,16,256]{2,1,0:T(8,128)S(1)} %fusion.41) | copy-start | bytes 2555908
  125.0 37.0 %copy-start.2 = (f32[26,2,16,256]{3,2,1,0:T(8,128)S(1)}, f32[26,2,16,256]{3,2,1,0:T(8,128)}, u32[]{:S(2)}) copy-start(f32[26,2,16,256]{3,2,1,0:T(8,128)} %fusion.20) | copy-start | bytes 2555908
  125.4 10.3 %collective-permute-start.3 = (f32[18,52,16]{0,2,1:T(8,128)S(1)}, f32[18,52,16]{0,2,1:T(8,128)}, u32[]{:S(2)}, u32[]{:S(2)}) collective-permute-start(f32[18,52,16]{0,2,1:T(8,128)S(1)} %broadcast_select_fusion.4), channel_id=1, source_target_pairs={{4,0},{8,4},{12,8},{0,12},{5,1},{9,5},{13,9},{1,13},{6,2},{10,6},{... | collective-permute-start | bytes 179720 | tf_op jit(solution)/shard_map/ppermute | solution.py:18
  125.8 36.2 %collective-permute-start.4 = (f32[32,52,16]{0,2,1:T(8,128)S(1)}, f32[32,52,16]{0,2,1:T(8,128)}, u32[]{:S(2)}, u32[]{:S(2)}) collective-permute-start(f32[32,52,16]{0,2,1:T(8,128)S(1)} %broadcast_select_fusion.5), channel_id=1, source_target_pairs={{8,0},{12,4},{0,8},{4,12},{9,1},{13,5},{1,9},{5,13},{10,2},{14,6},... | collective-permute-start | bytes 319496 | tf_op jit(solution)/shard_map/ppermute | solution.py:18
  126.9 26.0 %collective-permute-start.5 = (f32[18,52,16]{0,2,1:T(8,128)S(1)}, f32[18,52,16]{0,2,1:T(8,128)S(1)}, u32[]{:S(2)}, u32[]{:S(2)}) collective-permute-start(f32[18,52,16]{0,2,1:T(8,128)S(1)} %broadcast_select_fusion.3), channel_id=1, source_target_pairs={{12,0},{0,4},{4,8},{8,12},{13,1},{1,5},{5,9},{9,13},{14,2},{2,6},{... | collective-permute-start | bytes 179720 | tf_op jit(solution)/shard_map/ppermute | solution.py:18
  187.6 14.9 %copy-start.3 = (f32[26,2,16,256]{3,2,1,0:T(8,128)S(1)}, f32[26,2,16,256]{3,2,1,0:T(8,128)}, u32[]{:S(2)}) copy-start(f32[26,2,16,256]{3,2,1,0:T(8,128)} %fusion.20) | copy-start | bytes 2555908
  187.6 14.9 %copy-start.13 = (f32[8,16,16,1]{1,2,0,3:T(8,128)S(1)}, f32[8,16,16,1]{1,2,0,3:T(8,128)}, u32[]{:S(2)}) copy-start(f32[8,16,16,1]{1,2,0,3:T(8,128)} %constant.203) | copy-start | bytes 24580
  202.5 6.0 %copy-start.5 = (f32[52,16,256]{2,1,0:T(8,128)S(1)}, f32[52,16,256]{2,1,0:T(8,128)}, u32[]{:S(2)}) copy-start(f32[52,16,256]{2,1,0:T(8,128)} %copy-done.4) | copy-start | bytes 2555908
  225.8 14.0 %copy-start.16 = (f32[16,256]{1,0:T(8,128)}, f32[16,256]{1,0:T(8,128)S(1)}, u32[]{:S(2)}) copy-start(f32[16,256]{1,0:T(8,128)S(1)} %psum.7) | copy-start | bytes 49156
  226.0 9.1 %collective-permute-start.6 = (f32[25,1,16,256]{3,2,1,0:T(8,128)S(1)}, f32[25,1,16,256]{3,2,1,0:T(8,128)S(1)}, u32[]{:S(2)}, u32[]{:S(2)}) collective-permute-start(f32[25,1,16,256]{3,2,1,0:T(8,128)S(1)} %get-tuple-element.55), channel_id=1, source_target_pairs={{0,1},{1,2},{2,3},{4,5},{5,6},{6,7},{8,9},{9,10},{10,11},{12,13},{... | collective-permute-start | bytes 1228808 | tf_op jit(solution)/shard_map/ppermute | solution.py:40
  230.2 9.3 %collective-permute-start.7 = (f32[25,1,16,256]{3,2,1,0:T(8,128)S(1)}, f32[25,1,16,256]{3,2,1,0:T(8,128)S(1)}, u32[]{:S(2)}, u32[]{:S(2)}) collective-permute-start(f32[25,1,16,256]{3,2,1,0:T(8,128)S(1)} %get-tuple-element.54), channel_id=1, source_target_pairs={{1,0},{2,1},{3,2},{5,4},{6,5},{7,6},{9,8},{10,9},{11,10},{13,12},{... | collective-permute-start | bytes 1228808 | tf_op jit(solution)/shard_map/ppermute | solution.py:42
  (12 other events, 25.8 us)
where the time goes:
time: 242 us; the launch traced here: 241 us
  local copies, waits for them, and re-layouts  131 us (54%)
  waiting for transfers between devices  41.3 us (17%)
  other arithmetic  18.7 us (8%)
  blocking collectives  16.9 us (7%)
  matrix products  16.7 us (7%)
  starting transfers between devices  14.6 us (6%)
    gather x4, local copies, waits for them, and re-layouts, assemble_rows(): picked = jnp.take(extended, flat_index, axis=0).reshape((8,) + rows.shape)  71.2 us
    gather x3, local copies, waits for them, and re-layouts, per_device(): positions = jnp.where(relation == peer, start + rank[within], positions)  39.4 us
    ppermute x6, waiting for transfers between devices, shifted(): return lax.ppermute(block, axis, route)  34.1 us
    dot_general x2, matrix products, assemble_rows(): jnp.einsum('dwfm,dmn->wfn', picked, jnp.asarray(link_table()), precision=...  12.1 us
    psum x1, blocking collectives, per_device(): surface = lax.psum(column, 'lev')  9.44 us
    ppermute x6, starting transfers between devices, shifted(): return lax.ppermute(block, axis, route)  8.5 us
    all_gather x1, blocking collectives, prefix(): gathered = lax.all_gather(part, axis)  7.44 us
    gather x12, local copies, waits for them, and re-layouts, extend(): packed = jnp.take(rows, order, axis=0)  7.08 us
  transfers between devices with their start and end apart: 8, of which 5 were waited for; matrix products, arithmetic and copies ran while one was open for 21% of the time, Pallas kernels for 0%

commit v1 on v0

v1 whole, which is shorter than its diff:
```python
import functools
import math

import jax
import jax.numpy as jnp
import numpy as np
from jax import lax
from jax.experimental import pallas as pl
from jax.experimental.pallas import tpu as pltpu
from jax.sharding import PartitionSpec as P

PSIDE = 16
STEP = 0.035
MESH = pl.DeviceIdType.MESH
F32 = jnp.float32
BF16 = jnp.bfloat16

SOURCE = [[0, 4, 8, 12], [3, 7, 11, 15], [0, 1, 2, 3], [12, 13, 14, 15], [0], [3], [12], [15]]
TARGET = [[3, 7, 11, 15], [0, 4, 8, 12], [12, 13, 14, 15], [0, 1, 2, 3], [15], [12], [3], [0]]
OPPOSITE = [1, 0, 3, 2, 7, 6, 5, 4]


def lagrange_scale(points, which):
    product = 1.0
    for other in range(4):
        if other != which:
            product = product * (points[which] - points[other])
    return product


def node_tables():
    points = [-1.0, -1.0 / math.sqrt(5.0), 1.0 / math.sqrt(5.0), 1.0]
    weights = [1.0 / 6.0, 5.0 / 6.0, 5.0 / 6.0, 1.0 / 6.0]
    derivative = np.zeros((4, 4))
    for target in range(4):
        for source in range(4):
            if target == source:
                derivative[target, source] = sum(
                    1.0 / (points[target] - points[other]) for other in range(4) if other != target
                )
            else:
                derivative[target, source] = lagrange_scale(points, target) / (
                    lagrange_scale(points, source) * (points[target] - points[source])
                )
    derivative[np.abs(derivative) < 1e-12] = 0.0
    return derivative, weights


def plan(count):
    across = min(8, max(2, count // 8))
    offsets = [1, -1, across, -across, across + 1, across - 1, 1 - across, -1 - across]
    groups = {}
    for direction, offset in enumerate(offsets):
        groups.setdefault(offset % count, []).append(direction)
    keys = sorted(groups)
    lanes = {}
    for key in keys:
        start = 0
        for direction in groups[key]:
            lanes[direction] = start
            start += 4 * PSIDE if direction < 4 else 1
        assert start <= 128
    return offsets, keys, groups, lanes


def kernel(
    count, nlev, ntrc,
    tr, lm, wind, met, nb, nbt,
    out, surf,
    x0, x1, acc, gat, pck, upk, flag, msg, got, coef, thick, last, column, columns,
    rdn, rup, rlo, rhi, edn, eup, elo, ehi, delta, inv,
    halo_send, halo_recv, col_send, col_recv, up_send, up_recv, dn_send, dn_recv,
):
    width = met.shape[1]
    offsets, keys, groups, lanes = plan(count)
    ngroups = len(keys)
    place = lax.axis_index("elem")
    level = lax.axis_index("lev")
    main = ntrc - 1
    half = 32
    derivative, weights = node_tables()

    rlo[...] = jnp.zeros_like(rlo)
    rhi[...] = jnp.zeros_like(rhi)
    elo[...] = jnp.zeros_like(elo)
    ehi[...] = jnp.zeros_like(ehi)

    barrier = pltpu.get_barrier_semaphore()
    for key in keys:
        pl.semaphore_signal(
            barrier, inc=1, device_id={"elem": lax.rem(place + key, count)}, device_id_type=MESH
        )
    for turn in range(1, nlev):
        pl.semaphore_signal(
            barrier, inc=1, device_id={"lev": lax.rem(level + turn, nlev)}, device_id_type=MESH
        )

    for node in range(16):
        for lev in range(2):
            at = lev * 16 + node
            thin = lm[at : at + 1, :]
            x0[node, lev * half : lev * half + main, :] = (
                tr[0:main, lev, node, :] * thin
            )
            x0[node, lev * half + main : lev * half + half, :] = jnp.zeros(
                (half - main, width), F32
            )
            x0[node, lev * half + main : lev * half + main + 1, :] = (
                tr[main, lev, node : node + 1, :] * thin
            )
            x0[node, lev * half + ntrc : lev * half + ntrc + 1, :] = thin

    sub = lax.broadcasted_iota(jnp.int32, (width, width), 0)
    lane = lax.broadcasted_iota(jnp.int32, (width, width), 1)
    for d in range(8):
        base = lax.rem(place + offsets[d] % count, count) * width
        row = nbt[d : d + 1, :] - base
        frow = (row >= 0) & (row < width)
        flag[d : d + 1, :] = jnp.where(frow, 1.0, 0.0)
        if d >= 4:
            continue
        col = nb[:, d : d + 1] - base
        fcol = (col >= 0) & (col < width)
        own = nbt[d : d + 1, :] - place * width
        gat[d] = jnp.where(sub == own, 1.0, 0.0).astype(BF16)
        placed = jnp.where(fcol, col, 2 * width)
        rank = jnp.sum(jnp.where(placed < row, 1.0, 0.0), axis=0, keepdims=True)
        rank = jnp.where(frow, rank, -1.0)
        slot = (lax.broadcasted_iota(jnp.int32, (128, width), 0) & (PSIDE - 1)).astype(F32)
        upk[d] = jnp.where(slot == rank, 1.0, 0.0).astype(BF16)
        order = jnp.sum(
            jnp.where(lane < sub, jnp.where(frow, 1.0, 0.0), 0.0), axis=1, keepdims=True
        )
        order = jnp.where(fcol, order, -1.0)
        slot = (lax.broadcasted_iota(jnp.int32, (width, 128), 1) & (PSIDE - 1)).astype(F32)
        pck[OPPOSITE[d]] = jnp.where(slot == order, 1.0, 0.0).astype(BF16)

    def spread(planes, table):
        rows = planes[0].shape[0]
        x = planes[0] if len(planes) == 1 else jnp.concatenate(planes, axis=0)
        high = x.astype(BF16)
        low = (x - high.astype(F32)).astype(BF16)
        y = jnp.dot(jnp.concatenate([high, low], axis=0), table, preferred_element_type=F32)
        y = y[: x.shape[0]] + y[x.shape[0] :]
        return [y[rows * i : rows * (i + 1)] for i in range(len(planes))]

    def weighted(state):
        def chunk(r, carry):
            lev = r // 4
            rows = pl.ds(pl.multiple_of(r * 8, 8), 8)
            total = [None] * 16

            def put(n, value):
                total[n] = value if total[n] is None else total[n] + value

            for n in range(16):
                i, j = n % 4, n // 4
                h = state[n, rows, :] * met[n : n + 1, :]
                f = h * wind[pl.ds(lev * 16 + n, 1), :]
                g = h * wind[pl.ds(32 + lev * 16 + n, 1), :]
                for a in range(4):
                    east = -weights[a] * weights[j] * derivative[a, i]
                    if east != 0.0:
                        put(4 * j + a, f * np.float32(east))
                    north = -weights[i] * weights[a] * derivative[a, j]
                    if north != 0.0:
                        put(4 * a + i, g * np.float32(north))
            for n in range(16):
                acc[n, rows, :] = total[n]
            return carry

        lax.fori_loop(0, 8, chunk, 0)

    lanes128 = lax.broadcasted_iota(jnp.int32, (64, 128), 1)

    def assemble(stage):
        for pair in ((0, 1), (2, 3)):
            ys = [spread([acc[n] for n in SOURCE[d]], gat[d]) for d in pair]
            for d, y in zip(pair, ys):
                for n, v in zip(TARGET[d], y):
                    acc[n] = acc[n] + v
        if stage == 0:
            pl.semaphore_wait(barrier, ngroups + nlev - 1)
        copies = []
        for g, key in enumerate(keys):
            total = jnp.zeros((64, 128), F32)
            for d in groups[key]:
                if d < 4:
                    y = spread([acc[n] for n in SOURCE[d]], pck[d])
                    for j in range(4):
                        group = lanes[d] // PSIDE + j
                        total = jnp.where(lanes128 // PSIDE == group, y[j], total)
                else:
                    o = OPPOSITE[d]
                    value = jnp.sum(acc[SOURCE[d][0]] * flag[o : o + 1, :], axis=1, keepdims=True)
                    total = jnp.where(lanes128 == lanes[d], value, total)
            msg[stage, g] = total
            copy = pltpu.make_async_remote_copy(
                src_ref=msg.at[stage, g],
                dst_ref=got.at[stage, g],
                send_sem=halo_send.at[stage, g],
                recv_sem=halo_recv.at[stage, g],
                device_id={"elem": lax.rem(place + count - key, count)},
                device_id_type=MESH,
            )
            copy.start()
            copies.append(copy)
        for g, key in enumerate(keys):
            copies[g].wait()
            arrived = got[stage, g]
            for d in groups[key]:
                if d < 4:
                    first = lanes[d] // PSIDE
                    parts = [
                        jnp.where(lanes128 // PSIDE == first + j, arrived, 0.0) for j in range(4)
                    ]
                    for n, v in zip(TARGET[d], spread(parts, upk[d])):
                        acc[n] = acc[n] + v
                else:
                    n = TARGET[d][0]
                    at = lanes[d]
                    acc[n] = acc[n] + arrived[:, at : at + 1] * flag[d : d + 1, :]

    weighted(x0)
    for n in range(16):
        w = np.float32(weights[n % 4] * weights[n // 4])
        acc[n, ntrc + 1 : ntrc + 2, :] = met[n : n + 1, :] * w
    assemble(0)
    for n in range(16):
        c = STEP / acc[n, ntrc + 1 : ntrc + 2, :]
        coef[n : n + 1, :] = c
        x1[n] = x0[n] + c * acc[n]
    weighted(x1)
    assemble(1)

    for n in range(16):
        final = 0.5 * (x0[n] + x1[n] + coef[n : n + 1, :] * acc[n])
        x1[n] = final
        for lev in range(2):
            last[lev, n : n + 1, :] = final[lev * half + main : lev * half + ntrc]
            thick[lev, n : n + 1, :] = final[lev * half + ntrc : lev * half + ntrc + 1]

    column[...] = thick[0] + thick[1]
    columns[level] = thick[0] + thick[1]
    col_copies = []
    for turn in range(1, nlev):
        copy = pltpu.make_async_remote_copy(
            src_ref=column,
            dst_ref=columns.at[level],
            send_sem=col_send.at[turn - 1],
            recv_sem=col_recv.at[turn - 1],
            device_id={"lev": lax.rem(level + turn, nlev)},
            device_id_type=MESH,
        )
        copy.start()
        col_copies.append(copy)

    def up_copy(q):
        src, dst = (eup, elo) if q == 4 else (rup.at[pl.ds(4 * q, 4)], rlo.at[pl.ds(4 * q, 4)])
        return pltpu.make_async_remote_copy(
            src_ref=src, dst_ref=dst, send_sem=up_send.at[q], recv_sem=up_recv.at[q],
            device_id={"lev": lax.rem(level + 1, nlev)}, device_id_type=MESH,
        )

    def dn_copy(q):
        src, dst = (edn, ehi) if q == 4 else (rdn.at[pl.ds(4 * q, 4)], rhi.at[pl.ds(4 * q, 4)])
        return pltpu.make_async_remote_copy(
            src_ref=src, dst_ref=dst, send_sem=dn_send.at[q], recv_sem=dn_recv.at[q],
            device_id={"lev": lax.rem(level + nlev - 1, nlev)}, device_id_type=MESH,
        )

    def when_up(fn):
        pl.when(level < nlev - 1)(fn)

    def when_dn(fn):
        pl.when(level > 0)(fn)

    inverse = [1.0 / thick[0], 1.0 / thick[1]]
    edn[...] = last[0] * inverse[0]
    eup[...] = last[1] * inverse[1]
    for q in range(5):
        if q < 4:
            for n in range(4 * q, 4 * q + 4):
                rdn[n] = x1[n, 0:main, :] * inverse[0][n : n + 1]
                rup[n] = x1[n, half : half + main, :] * inverse[1][n : n + 1]
        when_up(lambda: up_copy(q).start())
        when_dn(lambda: dn_copy(q).start())

    for copy in col_copies:
        copy.wait()
    below = jnp.zeros((16, width), F32)
    whole = jnp.zeros((16, width), F32)
    for lev in range(nlev):
        part = columns[lev]
        whole = whole + part
        below = below + jnp.where(lev < level, part, 0.0)
    surf[...] = whole
    nl = 2 * nlev
    above = [below, below + thick[0], below + thick[0] + thick[1]]
    for k in range(3):
        edge = (2 * level + k).astype(F32)
        fraction = (edge + edge * (edge - 1.0) * (1.0 / (nl - 1))) * (1.0 / (2.0 * nl))
        delta[k] = above[k] - whole * fraction
        if k < 2:
            share = (1.0 + 2.0 * edge * (1.0 / (nl - 1))) * (1.0 / (2.0 * nl))
            inv[k] = 1.0 / (whole * share)

    def remap(d, r, carried, scale):
        flux = [d[k] * jnp.where(d[k] > 0.0, r[k], r[k + 1]) for k in range(3)]
        return [(carried[k] + flux[k] - flux[k + 1]) * scale[k] for k in range(2)]

    for q in range(5):
        when_up(lambda: up_copy(q).wait_send())
        when_dn(lambda: dn_copy(q).wait_send())
        when_dn(lambda: up_copy(q).wait_recv())
        when_up(lambda: dn_copy(q).wait_recv())
        if q == 4:
            y = remap(
                [delta[k] for k in range(3)],
                [elo[...], edn[...], eup[...], ehi[...]],
                [last[0], last[1]],
                [inv[0], inv[1]],
            )
            out[main, 0] = y[0]
            out[main, 1] = y[1]
            continue
        for n in range(4 * q, 4 * q + 4):
            y = remap(
                [delta[k, n : n + 1, :] for k in range(3)],
                [rlo[n], rdn[n], rup[n], rhi[n]],
                [x1[n, 0:main, :], x1[n, half : half + main, :]],
                [inv[0, n : n + 1, :], inv[1, n : n + 1, :]],
            )
            out[0:main, 0, n, :] = y[0]
            out[0:main, 1, n, :] = y[1]


def solution(mesh):
    count, nlev = mesh.shape["elem"], mesh.shape["lev"]
    ngroups = len(plan(count)[1])

    def per_device(tracers, layer_mass, winds, metric, neighbours):
        ntrc, here, nodes, width = tracers.shape
        assert here == 2 and nodes == 16 and ntrc == 25
        main = ntrc - 1
        vmem = pl.BlockSpec(memory_space=pltpu.VMEM)
        dma = pltpu.SemaphoreType.DMA
        result, surface = pl.pallas_call(
            functools.partial(kernel, count, nlev, ntrc),
            out_shape=(
                jax.ShapeDtypeStruct(tracers.shape, F32),
                jax.ShapeDtypeStruct((nodes, width), F32),
            ),
            in_specs=[vmem] * 6,
            out_specs=(vmem, vmem),
            scratch_shapes=[
                pltpu.VMEM((nodes, 64, width), F32),
                pltpu.VMEM((nodes, 64, width), F32),
                pltpu.VMEM((nodes, 64, width), F32),
                pltpu.VMEM((4, width, width), BF16),
                pltpu.VMEM((4, width, 128), BF16),
                pltpu.VMEM((4, 128, width), BF16),
                pltpu.VMEM((8, width), F32),
                pltpu.VMEM((2, ngroups, 64, 128), F32),
                pltpu.VMEM((2, ngroups, 64, 128), F32),
                pltpu.VMEM((nodes, width), F32),
                pltpu.VMEM((2, nodes, width), F32),
                pltpu.VMEM((2, nodes, width), F32),
                pltpu.VMEM((nodes, width), F32),
                pltpu.VMEM((nlev, nodes, width), F32),
            ]
            + [pltpu.VMEM((nodes, main, width), F32)] * 4
            + [pltpu.VMEM((nodes, width), F32)] * 4
            + [
                pltpu.VMEM((3, nodes, width), F32),
                pltpu.VMEM((2, nodes, width), F32),
                dma((2, ngroups)),
                dma((2, ngroups)),
                dma((nlev - 1,)),
                dma((nlev - 1,)),
                dma((5,)),
                dma((5,)),
                dma((5,)),
                dma((5,)),
            ],
            compiler_params=pltpu.CompilerParams(collective_id=0, has_side_effects=True),
        )(
            tracers,
            layer_mass.reshape(-1, width),
            winds.reshape(-1, width),
            metric,
            neighbours,
            neighbours.T,
        )
        return result, surface

    placed = (
        P(None, "lev", None, ("members", "elem")),
        P("lev", None, ("members", "elem")),
        P(None, "lev", None, ("members", "elem")),
        P(None, "elem"),
        P("elem", None),
    )
    return jax.shard_map(
        per_device,
        mesh=mesh,
        in_specs=placed,
        out_specs=(P(None, "lev", None, ("members", "elem")), P(None, ("members", "elem"))),
        check_vma=False,
    )
```

time: 242 us -> 31.8 us (0.13)
  local copies, waits for them, and re-layouts: 131 us -> 4.22 us
  waiting for transfers between devices: 41.3 us -> 0 us
  Pallas kernels: 0 us -> 26.8 us
  other arithmetic: 18.7 us -> 0 us
  blocking collectives: 16.9 us -> 0 us
  matrix products: 16.7 us -> 0 us
  starting transfers between devices: 14.6 us -> 0 us
    gather x19 -> x0, local copies, waits for them, and re-layouts: 118 us -> none  [the longest x4 71.2 us: assemble_rows(): picked = jnp.take(extended, flat_index, axis=0).reshape((8,) + rows.shape)]
    ppermute x8 -> x0, waiting for transfers between devices: 41.3 us -> none  [the longest x6 34.1 us: shifted(): return lax.ppermute(block, axis, route)]
    pallas_call x0 -> x1, Pallas kernels: none -> 26.8 us  [per_device(): pl.pallas_call(functools.partial(kernel, count, nlev, ntrc), out_shape=(j...]
    dot_general x6 -> x0, matrix products: 16.7 us -> none  [the longest x2 12.1 us: assemble_rows(): jnp.einsum('dwfm,dmn->wfn', picked, jnp.asarray(link_table()), precision=...]
    ppermute x8 -> x0, starting transfers between devices: 14.6 us -> none  [the longest x6 8.5 us: shifted(): return lax.ppermute(block, axis, route)]
    psum x1 -> x0, blocking collectives: 9.44 us -> none  [per_device(): surface = lax.psum(column, 'lev')]
    all_gather x1 -> x0, blocking collectives: 7.44 us -> none  [prefix(): gathered = lax.all_gather(part, axis)]
    concatenate x2 -> x0, other arithmetic: 4.98 us -> none  [extend(): return jnp.concatenate(pieces, axis=0)]
  transfers between devices with their start and end apart: 8 -> 0, of which waited for: 5 -> 0; matrix products, arithmetic and copies ran while one was open for 21% -> 0% of each run, Pallas kernels for 0% -> 0%
where the time goes in v1:
time: 31.8 us; the launch traced here: 31.6 us
  Pallas kernels  26.8 us (84%)
  local copies, waits for them, and re-layouts  4.22 us (13%)
  between operations  0.65 us (2%)
    pallas_call x1, Pallas kernels, per_device(): pl.pallas_call(functools.partial(kernel, count, nlev, ntrc), out_shape=(j...  26.8 us
    unnamed x5, local copies, waits for them, and re-layouts  4.22 us

profile of v1, /device:TPU:1, one launch (start us, length us, event | category | flops | bytes accessed | tf_op | source)
XLA Modules:
  0.0 31.6 jit_solution(9655267134786593588)
XLA Ops:
  0.6 1.5 %copy.7.nb = s32[256,8]{1,0:T(8,128)} copy(s32[256,8]{0,1:T(8,128)} %param.9) | data formatting | bytes 16384 | tf_op args[4]
  2.1 26.8 %shard_map.68 = (f32[25,2,16,256]{3,2,1,0:T(8,128)}, f32[16,256]{1,0:T(8,128)}) custom-call(f32[25,2,16,256]{3,2,1,0:T(8,128)} %tr.1, f32[32,256]{1,0:T(8,128)} %bitcast.5, f32[64,256]{1,0:T(8,128)} %bitcast.3, f32[16,256]{1,0:T(8,128)} %met.1, s32[256,8]{1,0:T(8,128)} %copy.7.nb, s32[8,256]{1,0:T(8,128)} %bitcast.4), custom_call_target="tpu_custom_call" | custom-call | tf_op jit(solution)/shard_map/pallas_call | solution.py:348
  28.9 0.0 copy-start
  28.9 2.1 %copy.10 = f32[25,2,16,256]{3,2,1,0:T(8,128)} copy(f32[25,2,16,256]{3,2,1,0:T(8,128)} %get-tuple-element.4) | data formatting | bytes 1638400
  31.0 0.0 copy-done
  31.0 0.6 %copy.11 = f32[16,256]{1,0:T(8,128)} copy(f32[16,256]{1,0:T(8,128)S(1)} %copy-done) | data formatting | bytes 32768
Async XLA Ops:
  28.9 2.1 %copy-start = (f32[16,256]{1,0:T(8,128)S(1)}, f32[16,256]{1,0:T(8,128)}, u32[]{:S(2)}) copy-start(f32[16,256]{1,0:T(8,128)} %get-tuple-element.5) | copy-start | bytes 49156

commit v2 on v1

--- a/solution.py
+++ b/solution.py
@@ -65,11 +65,12 @@
 
 def kernel(
     count, nlev, ntrc,
-    tr, lm, wind, met, nb, nbt,
+    tr_hbm, lm, wind, met, nbt,
     out, surf,
-    x0, x1, acc, gat, pck, upk, flag, msg, got, coef, thick, last, column, columns,
-    rdn, rup, rlo, rhi, edn, eup, elo, ehi, delta, inv,
-    halo_send, halo_recv, col_send, col_recv, up_send, up_recv, dn_send, dn_recv,
+    tr, x0, x1, xn, acc, gat, pck, upk, flag, msg, got, gotn, coef, part, edge, elo, ehi,
+    column, columns, delta, inv, thin,
+    load_sem, halo_send, halo_recv, far_send, far_recv, col_send, col_recv,
+    up_send, up_recv, dn_send, dn_recv,
 ):
     width = met.shape[1]
     offsets, keys, groups, lanes = plan(count)
@@ -80,38 +81,38 @@
     half = 32
     derivative, weights = node_tables()
 
-    rlo[...] = jnp.zeros_like(rlo)
-    rhi[...] = jnp.zeros_like(rhi)
-    elo[...] = jnp.zeros_like(elo)
-    ehi[...] = jnp.zeros_like(ehi)
+    load = pltpu.make_async_copy(tr_hbm, tr, load_sem)
+    load.start()
+
+    xn[...] = jnp.zeros_like(xn)
+    gotn[...] = jnp.zeros_like(gotn)
+    for ref in (elo, ehi):
+        ref[0] = jnp.zeros((16, width), F32)
+        ref[1] = jnp.ones((16, width), F32)
 
     barrier = pltpu.get_barrier_semaphore()
     for key in keys:
         pl.semaphore_signal(
             barrier, inc=1, device_id={"elem": lax.rem(place + key, count)}, device_id_type=MESH
         )
+        for turn in (1, nlev - 1):
+            pl.semaphore_signal(
+                barrier,
+                inc=1,
+                device_id={
+                    "elem": lax.rem(place + key, count),
+                    "lev": lax.rem(level + turn, nlev),
+                },
+                device_id_type=MESH,
+            )
     for turn in range(1, nlev):
         pl.semaphore_signal(
             barrier, inc=1, device_id={"lev": lax.rem(level + turn, nlev)}, device_id_type=MESH
         )
 
-    for node in range(16):
-        for lev in range(2):
-            at = lev * 16 + node
-            thin = lm[at : at + 1, :]
-            x0[node, lev * half : lev * half + main, :] = (
-                tr[0:main, lev, node, :] * thin
-            )
-            x0[node, lev * half + main : lev * half + half, :] = jnp.zeros(
-                (half - main, width), F32
-            )
-            x0[node, lev * half + main : lev * half + main + 1, :] = (
-                tr[main, lev, node : node + 1, :] * thin
-            )
-            x0[node, lev * half + ntrc : lev * half + ntrc + 1, :] = thin
-
     sub = lax.broadcasted_iota(jnp.int32, (width, width), 0)
     lane = lax.broadcasted_iota(jnp.int32, (width, width), 1)
+    nb = jnp.transpose(nbt[...].astype(F32)).astype(jnp.int32)
     for d in range(8):
         base = lax.rem(place + offsets[d] % count, count) * width
         row = nbt[d : d + 1, :] - base
@@ -135,6 +136,22 @@
         slot = (lax.broadcasted_iota(jnp.int32, (width, 128), 1) & (PSIDE - 1)).astype(F32)
         pck[OPPOSITE[d]] = jnp.where(slot == order, 1.0, 0.0).astype(BF16)
 
+    load.wait()
+    for node in range(16):
+        for lev in range(2):
+            at = lev * 16 + node
+            mass = lm[at : at + 1, :]
+            x0[node, lev * half : lev * half + main, :] = (
+                tr[0:main, lev, node, :] * mass
+            )
+            x0[node, lev * half + main : lev * half + half, :] = jnp.zeros(
+                (half - main, width), F32
+            )
+            x0[node, lev * half + main : lev * half + main + 1, :] = (
+                tr[main, lev, node : node + 1, :] * mass
+            )
+            x0[node, lev * half + ntrc : lev * half + ntrc + 1, :] = mass
+
     def spread(planes, table):
         rows = planes[0].shape[0]
         x = planes[0] if len(planes) == 1 else jnp.concatenate(planes, axis=0)
@@ -173,15 +190,43 @@
 
     lanes128 = lax.broadcasted_iota(jnp.int32, (64, 128), 1)
 
-    def assemble(stage):
+    def gather():
         for pair in ((0, 1), (2, 3)):
             ys = [spread([acc[n] for n in SOURCE[d]], gat[d]) for d in pair]
             for d, y in zip(pair, ys):
                 for n, v in zip(TARGET[d], y):
                     acc[n] = acc[n] + v
-        if stage == 0:
-            pl.semaphore_wait(barrier, ngroups + nlev - 1)
-        copies = []
+
+    def halo_copy(stage, g):
+        return pltpu.make_async_remote_copy(
+            src_ref=msg.at[stage, g],
+            dst_ref=got.at[stage, g],
+            send_sem=halo_send.at[stage, g],
+            recv_sem=halo_recv.at[stage, g],
+            device_id={"elem": lax.rem(place + count - keys[g], count)},
+            device_id_type=MESH,
+        )
+
+    def far_copy(g, up):
+        return pltpu.make_async_remote_copy(
+            src_ref=msg.at[1, g, pl.ds(half * up, half)],
+            dst_ref=gotn.at[g, pl.ds(half * (1 - up), half)],
+            send_sem=far_send.at[g, up],
+            recv_sem=far_recv.at[g, up],
+            device_id={
+                "elem": lax.rem(place + count - keys[g], count),
+                "lev": lax.rem(level + (1 if up else nlev - 1), nlev),
+            },
+            device_id_type=MESH,
+        )
+
+    def when_up(fn):
+        pl.when(level < nlev - 1)(fn)
+
+    def when_dn(fn):
+        pl.when(level > 0)(fn)
+
+    def send(stage):
         for g, key in enumerate(keys):
             total = jnp.zeros((64, 128), F32)
             for d in groups[key]:
@@ -195,51 +240,100 @@
                     value = jnp.sum(acc[SOURCE[d][0]] * flag[o : o + 1, :], axis=1, keepdims=True)
                     total = jnp.where(lanes128 == lanes[d], value, total)
             msg[stage, g] = total
-            copy = pltpu.make_async_remote_copy(
-                src_ref=msg.at[stage, g],
-                dst_ref=got.at[stage, g],
-                send_sem=halo_send.at[stage, g],
-                recv_sem=halo_recv.at[stage, g],
-                device_id={"elem": lax.rem(place + count - key, count)},
-                device_id_type=MESH,
-            )
-            copy.start()
-            copies.append(copy)
+            halo_copy(stage, g).start()
+
+    def receive(arrived, fresh):
+        seen = set()
         for g, key in enumerate(keys):
-            copies[g].wait()
-            arrived = got[stage, g]
             for d in groups[key]:
                 if d < 4:
                     first = lanes[d] // PSIDE
                     parts = [
-                        jnp.where(lanes128 // PSIDE == first + j, arrived, 0.0) for j in range(4)
+                        jnp.where(lanes128 // PSIDE == first + j, arrived[g], 0.0)
+                        for j in range(4)
                     ]
-                    for n, v in zip(TARGET[d], spread(parts, upk[d])):
-                        acc[n] = acc[n] + v
+                    values = spread(parts, upk[d])
                 else:
-                    n = TARGET[d][0]
                     at = lanes[d]
-                    acc[n] = acc[n] + arrived[:, at : at + 1] * flag[d : d + 1, :]
+                    values = [arrived[g][:, at : at + 1] * flag[d : d + 1, :]]
+                for n, v in zip(TARGET[d], values):
+                    acc[n] = v if fresh and n not in seen else acc[n] + v
+                    seen.add(n)
 
     weighted(x0)
     for n in range(16):
         w = np.float32(weights[n % 4] * weights[n // 4])
         acc[n, ntrc + 1 : ntrc + 2, :] = met[n : n + 1, :] * w
-    assemble(0)
+    gather()
+    pl.semaphore_wait(barrier, 3 * ngroups + nlev - 1)
+    send(0)
+    for g in range(ngroups):
+        halo_copy(0, g).wait()
+    receive([got[0, g] for g in range(ngroups)], False)
     for n in range(16):
         c = STEP / acc[n, ntrc + 1 : ntrc + 2, :]
         coef[n : n + 1, :] = c
         x1[n] = x0[n] + c * acc[n]
     weighted(x1)
-    assemble(1)
+    gather()
+    send(1)
+    for g in range(ngroups):
+        when_up(lambda: far_copy(g, 1).start())
+        when_dn(lambda: far_copy(g, 0).start())
 
     for n in range(16):
-        final = 0.5 * (x0[n] + x1[n] + coef[n : n + 1, :] * acc[n])
-        x1[n] = final
+        ch = coef[n : n + 1, :] * 0.5
+        coef[n : n + 1, :] = ch
+        local = 0.5 * (x0[n] + x1[n]) + ch * acc[n]
+        x1[n] = local
         for lev in range(2):
-            last[lev, n : n + 1, :] = final[lev * half + main : lev * half + ntrc]
-            thick[lev, n : n + 1, :] = final[lev * half + ntrc : lev * half + ntrc + 1]
-
+            for k in range(2):
+                row = lev * half + main + k
+                edge[lev, k, n : n + 1, :] = local[row : row + 1]
+
+    def up_copy(q):
+        nodes = pl.ds(4 * q, 4)
+        src, dst = (
+            (edge.at[1], elo)
+            if q == 4
+            else (x1.at[nodes, pl.ds(half, main)], xn.at[nodes, pl.ds(0, main)])
+        )
+        return pltpu.make_async_remote_copy(
+            src_ref=src, dst_ref=dst, send_sem=up_send.at[q], recv_sem=up_recv.at[q],
+            device_id={"lev": lax.rem(level + 1, nlev)}, device_id_type=MESH,
+        )
+
+    def dn_copy(q):
+        nodes = pl.ds(4 * q, 4)
+        src, dst = (
+            (edge.at[0], ehi)
+            if q == 4
+            else (x1.at[nodes, pl.ds(0, main)], xn.at[nodes, pl.ds(half, main)])
+        )
+        return pltpu.make_async_remote_copy(
+            src_ref=src, dst_ref=dst, send_sem=dn_send.at[q], recv_sem=dn_recv.at[q],
+            device_id={"lev": lax.rem(level + nlev - 1, nlev)}, device_id_type=MESH,
+        )
+
+    for q in (4, 0, 1, 2, 3):
+        when_up(lambda: up_copy(q).start())
+        when_dn(lambda: dn_copy(q).start())
+
+    for g in range(ngroups):
+        halo_copy(1, g).wait()
+    receive([got[1, g] for g in range(ngroups)], True)
+    inner = (5, 6, 9, 10)
+    for n in range(16):
+        if n in inner:
+            x0[n] = x1[n]
+        else:
+            x0[n] = x1[n] + coef[n : n + 1, :] * acc[n]
+        for lev in range(2):
+            for k in range(2):
+                row = lev * half + main + k
+                part[lev, k, n : n + 1, :] = x0[n, row : row + 1, :]
+
+    thick = [part[0, 1], part[1, 1]]
     column[...] = thick[0] + thick[1]
     columns[level] = thick[0] + thick[1]
     col_copies = []
@@ -255,80 +349,76 @@
         copy.start()
         col_copies.append(copy)
 
-    def up_copy(q):
-        src, dst = (eup, elo) if q == 4 else (rup.at[pl.ds(4 * q, 4)], rlo.at[pl.ds(4 * q, 4)])
-        return pltpu.make_async_remote_copy(
-            src_ref=src, dst_ref=dst, send_sem=up_send.at[q], recv_sem=up_recv.at[q],
-            device_id={"lev": lax.rem(level + 1, nlev)}, device_id_type=MESH,
-        )
-
-    def dn_copy(q):
-        src, dst = (edn, ehi) if q == 4 else (rdn.at[pl.ds(4 * q, 4)], rhi.at[pl.ds(4 * q, 4)])
-        return pltpu.make_async_remote_copy(
-            src_ref=src, dst_ref=dst, send_sem=dn_send.at[q], recv_sem=dn_recv.at[q],
-            device_id={"lev": lax.rem(level + nlev - 1, nlev)}, device_id_type=MESH,
-        )
-
-    def when_up(fn):
-        pl.when(level < nlev - 1)(fn)
-
-    def when_dn(fn):
-        pl.when(level > 0)(fn)
-
-    inverse = [1.0 / thick[0], 1.0 / thick[1]]
-    edn[...] = last[0] * inverse[0]
-    eup[...] = last[1] * inverse[1]
-    for q in range(5):
-        if q < 4:
-            for n in range(4 * q, 4 * q + 4):
-                rdn[n] = x1[n, 0:main, :] * inverse[0][n : n + 1]
-                rup[n] = x1[n, half : half + main, :] * inverse[1][n : n + 1]
-        when_up(lambda: up_copy(q).start())
-        when_dn(lambda: dn_copy(q).start())
+    for g in range(ngroups):
+        when_up(lambda: far_copy(g, 1).wait_send())
+        when_dn(lambda: far_copy(g, 0).wait_send())
+        when_dn(lambda: far_copy(g, 1).wait_recv())
+        when_up(lambda: far_copy(g, 0).wait_recv())
+    receive([gotn[g] for g in range(ngroups)], True)
+    for n in inner:
+        acc[n] = jnp.zeros((64, width), F32)
 
     for copy in col_copies:
         copy.wait()
     below = jnp.zeros((16, width), F32)
     whole = jnp.zeros((16, width), F32)
     for lev in range(nlev):
-        part = columns[lev]
-        whole = whole + part
-        below = below + jnp.where(lev < level, part, 0.0)
+        piece = columns[lev]
+        whole = whole + piece
+        below = below + jnp.where(lev < level, piece, 0.0)
     surf[...] = whole
     nl = 2 * nlev
     above = [below, below + thick[0], below + thick[0] + thick[1]]
     for k in range(3):
-        edge = (2 * level + k).astype(F32)
-        fraction = (edge + edge * (edge - 1.0) * (1.0 / (nl - 1))) * (1.0 / (2.0 * nl))
+        place_k = (2 * level + k).astype(F32)
+        fraction = (place_k + place_k * (place_k - 1.0) * (1.0 / (nl - 1))) * (1.0 / (2.0 * nl))
         delta[k] = above[k] - whole * fraction
         if k < 2:
-            share = (1.0 + 2.0 * edge * (1.0 / (nl - 1))) * (1.0 / (2.0 * nl))
+            share = (1.0 + 2.0 * place_k * (1.0 / (nl - 1))) * (1.0 / (2.0 * nl))
             inv[k] = 1.0 / (whole * share)
 
     def remap(d, r, carried, scale):
         flux = [d[k] * jnp.where(d[k] > 0.0, r[k], r[k + 1]) for k in range(3)]
         return [(carried[k] + flux[k] - flux[k + 1]) * scale[k] for k in range(2)]
 
-    for q in range(5):
+    for q in (4, 0, 1, 2, 3):
         when_up(lambda: up_copy(q).wait_send())
         when_dn(lambda: dn_copy(q).wait_send())
         when_dn(lambda: up_copy(q).wait_recv())
         when_up(lambda: dn_copy(q).wait_recv())
         if q == 4:
+            tail = [[], []]
+            for side, ref in enumerate((elo, ehi)):
+                for k in range(2):
+                    row = side * half + main + k
+                    fix = jnp.concatenate([acc[n, row : row + 1, :] for n in range(16)], axis=0)
+                    tail[side].append(ref[k] + coef[...] * fix)
+            thin[0] = 1.0 / tail[0][1]
+            thin[1] = 1.0 / thick[0]
+            thin[2] = 1.0 / thick[1]
+            thin[3] = 1.0 / tail[1][1]
+            carried = [tail[0][0], part[0, 0], part[1, 0], tail[1][0]]
             y = remap(
                 [delta[k] for k in range(3)],
-                [elo[...], edn[...], eup[...], ehi[...]],
-                [last[0], last[1]],
+                [carried[k] * thin[k] for k in range(4)],
+                carried[1:3],
                 [inv[0], inv[1]],
             )
             out[main, 0] = y[0]
             out[main, 1] = y[1]
             continue
         for n in range(4 * q, 4 * q + 4):
+            ch = coef[n : n + 1, :]
+            carried = [
+                xn[n, 0:main, :] + ch * acc[n, 0:main, :],
+                x0[n, 0:main, :],
+                x0[n, half : half + main, :],
+                xn[n, half : half + main, :] + ch * acc[n, half : half + main, :],
+            ]
             y = remap(
                 [delta[k, n : n + 1, :] for k in range(3)],
-                [rlo[n], rdn[n], rup[n], rhi[n]],
-                [x1[n, 0:main, :], x1[n, half : half + main, :]],
+                [carried[k] * thin[k, n : n + 1, :] for k in range(4)],
+                carried[1:3],
                 [inv[0, n : n + 1, :], inv[1, n : n + 1, :]],
             )
             out[0:main, 0, n, :] = y[0]
@@ -351,31 +441,33 @@
                 jax.ShapeDtypeStruct(tracers.shape, F32),
                 jax.ShapeDtypeStruct((nodes, width), F32),
             ),
-            in_specs=[vmem] * 6,
+            in_specs=[pl.BlockSpec(memory_space=pl.ANY)] + [vmem] * 4,
             out_specs=(vmem, vmem),
-            scratch_shapes=[
-                pltpu.VMEM((nodes, 64, width), F32),
-                pltpu.VMEM((nodes, 64, width), F32),
-                pltpu.VMEM((nodes, 64, width), F32),
+            scratch_shapes=[pltpu.VMEM(tracers.shape, F32)]
+            + [pltpu.VMEM((nodes, 64, width), F32)] * 4
+            + [
                 pltpu.VMEM((4, width, width), BF16),
                 pltpu.VMEM((4, width, 128), BF16),
                 pltpu.VMEM((4, 128, width), BF16),
                 pltpu.VMEM((8, width), F32),
                 pltpu.VMEM((2, ngroups, 64, 128), F32),
                 pltpu.VMEM((2, ngroups, 64, 128), F32),
+                pltpu.VMEM((ngroups, 64, 128), F32),
                 pltpu.VMEM((nodes, width), F32),
+                pltpu.VMEM((2, 2, nodes, width), F32),
+                pltpu.VMEM((2, 2, nodes, width), F32),
                 pltpu.VMEM((2, nodes, width), F32),
                 pltpu.VMEM((2, nodes, width), F32),
                 pltpu.VMEM((nodes, width), F32),
                 pltpu.VMEM((nlev, nodes, width), F32),
-            ]
-            + [pltpu.VMEM((nodes, main, width), F32)] * 4
-            + [pltpu.VMEM((nodes, width), F32)] * 4
-            + [
                 pltpu.VMEM((3, nodes, width), F32),
                 pltpu.VMEM((2, nodes, width), F32),
+                pltpu.VMEM((4, nodes, width), F32),
+                dma,
                 dma((2, ngroups)),
                 dma((2, ngroups)),
+                dma((ngroups, 2)),
+                dma((ngroups, 2)),
                 dma((nlev - 1,)),
                 dma((nlev - 1,)),
                 dma((5,)),
@@ -389,7 +481,6 @@
             layer_mass.reshape(-1, width),
             winds.reshape(-1, width),
             metric,
-            neighbours,
             neighbours.T,
         )
         return result, surface

time: 31.8 us -> 29.2 us (0.918)
  the two profiles are of different devices: /device:TPU:1 before, /device:TPU:0 now
where the time goes in v2:
time: 29.2 us; the launch traced here: 29 us
  Pallas kernels  25.6 us (88%)
  local copies, waits for them, and re-layouts  2.73 us (9%)
  between operations  0.65 us (2%)
    pallas_call x1, Pallas kernels, per_device(): pl.pallas_call(functools.partial(kernel, count, nlev, ntrc), out_shape=(j...  25.6 us
    unnamed x4, local copies, waits for them, and re-layouts  2.73 us

profile of v2, /device:TPU:0, one launch (start us, length us, event | category | flops | bytes accessed | tf_op | source)
XLA Modules:
  0.0 29.0 jit_solution(10929739041424656886)
XLA Ops:
  0.6 25.6 %shard_map.68 = (f32[25,2,16,256]{3,2,1,0:T(8,128)}, f32[16,256]{1,0:T(8,128)}) custom-call(f32[25,2,16,256]{3,2,1,0:T(8,128)} %tr_hbm.1, f32[32,256]{1,0:T(8,128)} %bitcast.4, f32[64,256]{1,0:T(8,128)} %bitcast.3, f32[16,256]{1,0:T(8,128)} %met.1, s32[8,256]{1,0:T(8,128)} %bitcast.5), custom_call_target="tpu_custom_call" | custom-call | tf_op jit(solution)/shard_map/pallas_call | solution.py:438
  26.3 0.0 copy-start
  26.3 2.1 %copy.9 = f32[25,2,16,256]{3,2,1,0:T(8,128)} copy(f32[25,2,16,256]{3,2,1,0:T(8,128)} %get-tuple-element.4) | data formatting | bytes 1638400
  28.4 0.0 copy-done
  28.4 0.6 %copy.10 = f32[16,256]{1,0:T(8,128)} copy(f32[16,256]{1,0:T(8,128)S(1)} %copy-done) | data formatting | bytes 32768
Async XLA Ops:
  26.3 2.1 %copy-start = (f32[16,256]{1,0:T(8,128)S(1)}, f32[16,256]{1,0:T(8,128)}, u32[]{:S(2)}) copy-start(f32[16,256]{1,0:T(8,128)} %get-tuple-element.5) | copy-start | bytes 49156
